TPU v7x, 256 devices: a whole 4x4x8 slice. The times are simulated.
256 devices in a mesh: patch: 32 (over y, z), sub: 8 (over x, core).
Axes of the slice: x: 4, y: 4, z: 8, core: 2. Of those that a mesh axis runs over, the one named last changes fastest.
Arguments:
- heat: float32 [2097152], P(('patch', 'sub')), may hold values from -6 to 6
- basis: bfloat16 [9, 4194304], P(None, ('patch', 'sub')), may hold values from -3 to 3
- area: float32 [4194304], P(('patch', 'sub')), may hold values from 0.2 to 2
- corners: int32 [3, 4194304], P(None, ('patch', 'sub')), may hold values from 0 to 9215, as said below
- send_sub: int32 [16384], P(('patch', 'sub')), may hold values from 0 to 8191
- send_pat: int32 [4, 32768], P(None, ('patch', 'sub')), may hold values from 0 to 8191
- live_faces: int32 [256], P(('patch', 'sub')), may hold values from 12288 to 16384, as said below
Outputs:
- divergence: float32 [2097152], P(('patch', 'sub'))
Inputs may be any that keep to these rules, and one draw needn't show every extreme that they name: Face slot f of a device lies in tile t = f // 128; each of its corners is either an owned position in [64 t - 128, 64 t + 128) or a remote position from 8192 + 256 (t mod (4)) up to 255 beyond that; every position of the device's table is read by some face of the device. `live_faces`: some device has all 16384 slots live.
All inputs are finite; a program needn't handle non-finite values.
Results may differ from a plain program's by a relative error of at most 0.0003.
Values sent between devices are 32-bit elements; how exact they have to be, the bound alone decides.
A program may use at most 64 MiB of HBM per device.

v0:
```python
import jax
import jax.numpy as jnp
from jax import lax
from jax.sharding import PartitionSpec as P

RADIUS = 2


def in_order(blocks, dim):
    dims = list(blocks.shape[1:])
    dims[dim] *= blocks.shape[0]
    return jnp.moveaxis(blocks, 0, dim).reshape(dims)


def sent_to_all(x, axis):
    copies = jnp.broadcast_to(x, (lax.axis_size(axis), *x.shape))
    return lax.all_to_all(copies, axis, split_axis=0, concat_axis=0, tiled=True)


def gather_directly(x, axis, dim):
    return in_order(sent_to_all(x, axis), dim)


def from_behind(x, axis, by):
    length = lax.axis_size(axis)
    return lax.ppermute(x, axis, [(i, (i + by) % length) for i in range(length)])


def split_up(x, dim, length):
    dims = x.shape
    blocks = x.reshape(*dims[:dim], length, dims[dim] // length, *dims[dim + 1 :])
    return jnp.moveaxis(blocks, dim, 0)


def sent_and_summed(x, axis, dim):
    length = lax.axis_size(axis)
    blocks = lax.all_to_all(split_up(x, dim, length), axis, 0, 0, tiled=True)
    return jnp.sum(blocks, axis=0)


def offset_list():
    return [k + 1 for k in range(RADIUS)] + [-(k + 1) for k in range(RADIUS)]


def tile_terms(
    window,
    remote_window,
    corner_tile,
    basis_tile,
    area_tile,
    start,
    remote_start,
    first_slot,
    live_count,
):
    window_pos = jnp.arange(window.shape[0])
    remote_pos = jnp.arange(remote_window.shape[0])
    onehot_near = (corner_tile[:, :, None] - start == window_pos).astype(jnp.float32)
    onehot_far = (corner_tile[:, :, None] - remote_start == remote_pos).astype(jnp.float32)
    values = jnp.einsum("kfw,w->kf", onehot_near, window, precision=lax.Precision.HIGHEST)
    values = values + jnp.einsum(
        "kfw,w->kf", onehot_far, remote_window, precision=lax.Precision.HIGHEST
    )
    width = corner_tile.shape[1]
    gradients = basis_tile.astype(jnp.float32).reshape(3, 3, width)
    gradient = jnp.sum(gradients * values[:, None, :], axis=0)
    length = jnp.sqrt(jnp.sum(gradient * gradient, axis=0))
    field = -gradient / jnp.maximum(length, 1.0)
    projected = jnp.sum(gradients * field[None, :, :], axis=1)
    live_mask = first_slot + jnp.arange(width) < live_count
    weight = jnp.where(live_mask, area_tile, 0.0)
    terms = projected * weight[None, :]
    near_sums = jnp.einsum("kfw,kf->w", onehot_near, terms, precision=lax.Precision.HIGHEST)
    far_sums = jnp.einsum("kfw,kf->w", onehot_far, terms, precision=lax.Precision.HIGHEST)
    return (near_sums, far_sums)


def face_terms(heat, remote, corners, basis, area, live_count):
    owned = heat.shape[0]
    slots = corners.shape[1]
    tiles = slots // 128
    remote_len = remote.shape[0]
    remote_win = min(256, remote_len)
    remote_blocks = remote_len // remote_win
    padded = jnp.pad(heat, (128, 128))
    pieces = padded.reshape(tiles + 4, 64)
    windows = jnp.concatenate([pieces[shift : shift + tiles] for shift in range(4)], axis=1)
    remote_tiles = jnp.tile(remote.reshape(remote_blocks, remote_win), (tiles // remote_blocks, 1))
    tile_ids = jnp.arange(tiles)
    starts = 64 * tile_ids - 128
    remote_starts = owned + remote_win * (tile_ids % remote_blocks)
    first_slots = 128 * tile_ids
    corner_tiles = corners.reshape(3, tiles, 128).transpose(1, 0, 2)
    basis_tiles = basis.reshape(9, tiles, 128).transpose(1, 0, 2)
    area_tiles = area.reshape(tiles, 128)
    batch = 1
    limit = max(1, tiles // 16)
    while batch * 2 <= limit and tiles % (batch * 2) == 0:
        batch = batch * 2
    groups = tiles // batch
    packed = (
        windows,
        remote_tiles,
        corner_tiles,
        basis_tiles,
        area_tiles,
        starts,
        remote_starts,
        first_slots,
    )
    packed = jax.tree.map(lambda array: array.reshape((groups, batch) + array.shape[1:]), packed)

    def run_group(pack):
        return jax.vmap(
            lambda w, r, c, b, a, s, q, f: tile_terms(w, r, c, b, a, s, q, f, live_count)
        )(*pack)

    near_sums, far_sums = lax.map(run_group, packed)
    near_sums = near_sums.reshape(tiles, 4, 64)
    summed = jnp.zeros((tiles + 4, 64), jnp.float32)
    for shift in range(4):
        summed = summed + jnp.pad(near_sums[:, shift], ((shift, 4 - shift), (0, 0)))
    owned_sums = summed.reshape(-1)[128 : 128 + owned]
    far_sums = far_sums.reshape(tiles // remote_blocks, remote_blocks, remote_win)
    remote_sums = jnp.sum(far_sums, axis=0).reshape(-1)
    return (owned_sums, remote_sums)


def per_device(heat, basis, area, corners, send_sub, send_pat, live_faces):
    sub_count = lax.axis_size("sub")
    group_size = send_sub.shape[0]
    block_size = send_pat.shape[1]
    offsets = offset_list()
    group_send = jnp.take(heat, send_sub)
    group_values = gather_directly(group_send, "sub", 0)
    outgoing = jnp.take(heat, send_pat)
    incoming = jnp.stack(
        [
            from_behind(outgoing[block_index], "patch", offset)
            for block_index, offset in enumerate(offsets)
        ]
    )
    remote = jnp.concatenate([group_values, incoming.reshape(-1)])
    result, remote_sums = face_terms(heat, remote, corners, basis, area, live_faces[0])
    group_part = remote_sums[: sub_count * group_size]
    patch_part = remote_sums[sub_count * group_size :].reshape(2 * RADIUS, block_size)
    group_back = sent_and_summed(group_part, "sub", 0)
    returned = jnp.stack(
        [
            from_behind(patch_part[block_index], "patch", -offset)
            for block_index, offset in enumerate(offsets)
        ]
    )
    result = result.at[send_sub].add(group_back)
    result = result.at[send_pat.reshape(-1)].add(returned.reshape(-1))
    return result


def solution(mesh):
    placed = (
        P(("patch", "sub")),
        P(None, ("patch", "sub")),
        P(("patch", "sub")),
        P(None, ("patch", "sub")),
        P(("patch", "sub")),
        P(None, ("patch", "sub")),
        P(("patch", "sub")),
    )
    return jax.shard_map(
        per_device, mesh=mesh, in_specs=placed, out_specs=P(("patch", "sub")), check_vma=False
    )
```

profile of v0, /device:TPU:1, one launch (start us, length us, event | category | flops | bytes accessed | tf_op | source)
XLA Modules:
  0.0 190.9 jit_solution(4873083875064805291)
XLA Ops:
  0.7 3.5 %gather_fusion.1 = f32[512]{0:T(512)S(1)} fusion(f32[8192]{0:T(1024)} %param.9, s32[1024]{0:T(1024)S(1)} %pad_clamp_fusion), kind=kCustom, calls=%fused_computation.1 | custom fusion | bytes 6144 | tf_op jit(solution)/shard_map/jit(_take)/gather | solution.py:136
  4.3 2.5 %collective-permute-start = (f32[128]{0:T(128)S(1)}, f32[128]{0:T(128)S(1)}, u32[]{:S(2)}, u32[]{:S(2)}) collective-permute-start(f32[128]{0:T(128)S(1)} %get-tuple-element.135), channel_id=1, source_target_pairs={{0,8},{8,16},{16,24},{24,32},{32,40},{40,48},{48,56},{56,64},{64,7... | collective-permute-start | bytes 1544 | tf_op jit(solution)/shard_map/ppermute | solution.py:26
  6.8 3.0 %collective-permute-start.1 = (f32[128]{0:T(128)S(1)}, f32[128]{0:T(128)S(1)}, u32[]{:S(2)}, u32[]{:S(2)}) collective-permute-start(f32[128]{0:T(128)S(1)} %get-tuple-element.138), channel_id=1, source_target_pairs={{0,16},{8,24},{16,32},{24,40},{32,48},{40,56},{48,64},{56,72},{64,... | collective-permute-start | bytes 1544 | tf_op jit(solution)/shard_map/ppermute | solution.py:26
  9.8 3.6 %collective-permute-start.2 = (f32[128]{0:T(128)S(1)}, f32[128]{0:T(128)S(1)}, u32[]{:S(2)}, u32[]{:S(2)}) collective-permute-start(f32[128]{0:T(128)S(1)} %get-tuple-element.137), channel_id=1, source_target_pairs={{0,248},{8,0},{16,8},{24,16},{32,24},{40,32},{48,40},{56,48},{64,5... | collective-permute-start | bytes 1544 | tf_op jit(solution)/shard_map/ppermute | solution.py:26
  13.4 2.3 %collective-permute-start.3 = (f32[128]{0:T(128)S(1)}, f32[128]{0:T(128)S(1)}, u32[]{:S(2)}, u32[]{:S(2)}) collective-permute-start(f32[128]{0:T(128)S(1)} %get-tuple-element.136), channel_id=1, source_target_pairs={{0,240},{8,248},{16,0},{24,8},{32,16},{40,24},{48,32},{56,40},{64,... | collective-permute-start | bytes 1544 | tf_op jit(solution)/shard_map/ppermute | solution.py:26
  17.1 5.8 %all-to-all-start = ((f32[8,1,64]{2,1,0:T(1,128)}), f32[8,1,64]{2,1,0:T(1,128)S(1)}, u32[]{:S(2)}, u32[]{:S(2)}) async-start(f32[8,1,64]{2,1,0:T(1,128)} %broadcast_in_dim.48), calls=%async_computation | async-start | bytes 8192 | tf_op jit(solution)/shard_map/all_to_all | solution.py:17
  23.6 3.7 %all-to-all-done = f32[8,1,64]{2,1,0:T(1,128)S(1)} async-done(((f32[8,1,64]{2,1,0:T(1,128)}), f32[8,1,64]{2,1,0:T(1,128)S(1)}, u32[]{:S(2)}, u32[]{:S(2)}) %all-to-all-start) | async-done | bytes 2080 | tf_op jit(solution)/shard_map/all_to_all | solution.py:17
  28.7 140.8 %while.12 = (s32[]{:T(128)}, f32[16,8,256]{2,1,0:T(8,128)S(1)}, f32[16,8,256]{2,1,0:T(8,128)S(1)}, s32[16,8,3,128]{3,2,1,0:T(4,128)}, s32[16,8]{1,0:T(8,128)S(1)...) while((s32[]{:T(128)}, f32[16,8,256]{2,1,0:T(8,128)S(1)}, ...), condition=%wide.region_4.5_spmd, body=%wide.region_0.4_spmd.sunk | while | flops 40971264 | bytes 483781 | solution.py:118
  29.6 1.7 fusion.43
  31.3 1.7 fusion.44
  34.5 1.5 fusion.49
  36.0 1.5 fusion.48
  38.4 1.7 fusion.43
  40.1 1.7 fusion.44
  43.3 1.5 fusion.49
  44.8 1.5 fusion.48
  47.2 1.7 fusion.43
  48.9 1.7 fusion.44
  52.1 1.5 fusion.49
  53.6 1.5 fusion.48
  56.0 1.7 fusion.43
  57.7 1.7 fusion.44
  62.4 1.5 fusion.48
  64.8 1.7 fusion.43
  66.5 1.7 fusion.44
  71.2 1.5 fusion.48
  73.6 1.7 fusion.43
  75.3 1.7 fusion.44
  80.0 1.5 fusion.48
  82.4 1.7 fusion.43
  84.1 1.7 fusion.44
  88.8 1.5 fusion.48
  91.2 1.7 fusion.43
  92.9 1.7 fusion.44
  97.6 1.5 fusion.48
  100.0 1.7 fusion.43
  101.7 1.7 fusion.44
  106.4 1.5 fusion.48
  108.8 1.7 fusion.43
  110.5 1.7 fusion.44
  115.2 1.5 fusion.48
  117.6 1.7 fusion.43
  119.3 1.7 fusion.44
  124.0 1.5 fusion.48
  126.4 1.7 fusion.43
  128.1 1.7 fusion.44
  132.8 1.5 fusion.48
  135.2 1.7 fusion.43
  136.9 1.7 fusion.44
  141.6 1.5 fusion.48
  144.0 1.7 fusion.43
  145.7 1.7 fusion.44
  150.4 1.5 fusion.48
  152.8 1.7 fusion.43
  154.5 1.7 fusion.44
  159.2 1.5 fusion.48
  161.6 1.7 fusion.43
  163.3 1.7 fusion.44
  168.0 1.5 fusion.48
  170.0 1.7 collective-permute-start.4
  171.8 2.4 %collective-permute-start.5 = (f32[128]{0:T(128)S(1)}, f32[128]{0:T(128)S(1)}, u32[]{:S(2)}, u32[]{:S(2)}) collective-permute-start(f32[128]{0:T(128)S(1)} %get-tuple-element.134), channel_id=1, source_target_pairs={{0,240},{8,248},{16,0},{24,8},{32,16},{40,24},{48,32},{56,40},{64,... | collective-permute-start | bytes 1544 | tf_op jit(solution)/shard_map/ppermute | solution.py:26
  175.7 4.7 %all-to-all-start.1 = ((f32[8,1,64]{2,1,0:T(1,128)}), f32[8,1,64]{2,1,0:T(1,128)S(1)}, u32[]{:S(2)}, u32[]{:S(2)}) async-start(f32[8,1,64]{2,1,0:T(1,128)} %all_to_all.11), calls=%async_computation.1 | async-start | bytes 8192 | tf_op jit(solution)/shard_map/all_to_all | solution.py:37
  181.5 3.4 %all-to-all-done.1 = f32[8,1,64]{2,1,0:T(1,128)S(1)} async-done(((f32[8,1,64]{2,1,0:T(1,128)}), f32[8,1,64]{2,1,0:T(1,128)S(1)}, u32[]{:S(2)}, u32[]{:S(2)}) %all-to-all-start.1) | async-done | bytes 2080 | tf_op jit(solution)/shard_map/all_to_all | solution.py:37
  186.6 4.4 %scatter_fusion.1 = f32[8192]{0:T(1024)} fusion(f32[8192]{0:T(1024)} %copy-done.1, s32[512]{0:T(512)S(1)} %bitcast.127, f32[512]{0:T(512)S(1)} %maximum_bitcast_fusion), kind=kCustom, calls=%fused_computation.3 | custom fusion | flops 512 | bytes 8192 | tf_op jit(solution)/shard_map/scatter-add | solution.py:155
  (332 shorter events, 65.2 us)
Async XLA Ops:
  0.7 3.5 %copy-start.3 = (s32[4,128]{1,0:T(4,128)S(1)}, s32[4,128]{1,0:T(4,128)}, u32[]{:S(2)}) copy-start(s32[4,128]{1,0:T(4,128)} %param.14) | copy-start | bytes 6148
  0.7 14.9 %copy-start.4 = (s32[64]{0:T(128)S(1)}, s32[64]{0:T(128)}, u32[]{:S(2)}) copy-start(s32[64]{0:T(128)} %param.13) | copy-start | bytes 772
  0.7 14.9 %copy-start = (f32[8192]{0:T(1024)S(1)}, f32[8192]{0:T(1024)}, u32[]{:S(2)}) copy-start(f32[8192]{0:T(1024)} %param.9) | copy-start | bytes 98308
  4.3 19.3 %collective-permute-start = (f32[128]{0:T(128)S(1)}, f32[128]{0:T(128)S(1)}, u32[]{:S(2)}, u32[]{:S(2)}) collective-permute-start(f32[128]{0:T(128)S(1)} %get-tuple-element.135), channel_id=1, source_target_pairs={{0,8},{8,16},{16,24},{24,32},{32,40},{40,48},{48,56},{56,64},{64,7... | collective-permute-start | bytes 1544 | tf_op jit(solution)/shard_map/ppermute | solution.py:26
  6.8 16.8 %collective-permute-start.1 = (f32[128]{0:T(128)S(1)}, f32[128]{0:T(128)S(1)}, u32[]{:S(2)}, u32[]{:S(2)}) collective-permute-start(f32[128]{0:T(128)S(1)} %get-tuple-element.138), channel_id=1, source_target_pairs={{0,16},{8,24},{16,32},{24,40},{32,48},{40,56},{48,64},{56,72},{64,... | collective-permute-start | bytes 1544 | tf_op jit(solution)/shard_map/ppermute | solution.py:26
  9.8 13.8 %collective-permute-start.2 = (f32[128]{0:T(128)S(1)}, f32[128]{0:T(128)S(1)}, u32[]{:S(2)}, u32[]{:S(2)}) collective-permute-start(f32[128]{0:T(128)S(1)} %get-tuple-element.137), channel_id=1, source_target_pairs={{0,248},{8,0},{16,8},{24,16},{32,24},{40,32},{48,40},{56,48},{64,5... | collective-permute-start | bytes 1544 | tf_op jit(solution)/shard_map/ppermute | solution.py:26
  13.4 10.2 %collective-permute-start.3 = (f32[128]{0:T(128)S(1)}, f32[128]{0:T(128)S(1)}, u32[]{:S(2)}, u32[]{:S(2)}) collective-permute-start(f32[128]{0:T(128)S(1)} %get-tuple-element.136), channel_id=1, source_target_pairs={{0,240},{8,248},{16,0},{24,8},{32,16},{40,24},{48,32},{56,40},{64,... | collective-permute-start | bytes 1544 | tf_op jit(solution)/shard_map/ppermute | solution.py:26
  15.7 7.6 %copy-start.2 = (bf16[9,16384]{1,0:T(8,128)(2,1)S(1)}, bf16[9,16384]{1,0:T(8,128)(2,1)}, u32[]{:S(2)}) copy-start(bf16[9,16384]{1,0:T(8,128)(2,1)} %param.10) | copy-start | bytes 884740
  17.1 10.3 %all-to-all-start = ((f32[8,1,64]{2,1,0:T(1,128)}), f32[8,1,64]{2,1,0:T(1,128)S(1)}, u32[]{:S(2)}, u32[]{:S(2)}) async-start(f32[8,1,64]{2,1,0:T(1,128)} %broadcast_in_dim.48), calls=%async_computation | async-start | bytes 8192 | tf_op jit(solution)/shard_map/all_to_all | solution.py:17
  170.0 10.4 %collective-permute-start.4 = (f32[128]{0:T(128)S(1)}, f32[128]{0:T(128)S(1)}, u32[]{:S(2)}, u32[]{:S(2)}) collective-permute-start(f32[128]{0:T(128)S(1)} %get-tuple-element.131), channel_id=1, source_target_pairs={{0,248},{8,0},{16,8},{24,16},{32,24},{40,32},{48,40},{56,48},{64,5... | collective-permute-start | bytes 1544 | tf_op jit(solution)/shard_map/ppermute | solution.py:26
  171.8 8.7 %collective-permute-start.5 = (f32[128]{0:T(128)S(1)}, f32[128]{0:T(128)S(1)}, u32[]{:S(2)}, u32[]{:S(2)}) collective-permute-start(f32[128]{0:T(128)S(1)} %get-tuple-element.134), channel_id=1, source_target_pairs={{0,240},{8,248},{16,0},{24,8},{32,16},{40,24},{48,32},{56,40},{64,... | collective-permute-start | bytes 1544 | tf_op jit(solution)/shard_map/ppermute | solution.py:26
  174.1 6.3 %collective-permute-start.6 = (f32[128]{0:T(128)S(1)}, f32[128]{0:T(128)S(1)}, u32[]{:S(2)}, u32[]{:S(2)}) collective-permute-start(f32[128]{0:T(128)S(1)} %get-tuple-element.133), channel_id=1, source_target_pairs={{0,8},{8,16},{16,24},{24,32},{32,40},{40,48},{48,56},{56,64},{64,7... | collective-permute-start | bytes 1544 | tf_op jit(solution)/shard_map/ppermute | solution.py:26
  174.9 6.6 %collective-permute-start.7 = (f32[128]{0:T(128)S(1)}, f32[128]{0:T(128)S(1)}, u32[]{:S(2)}, u32[]{:S(2)}) collective-permute-start(f32[128]{0:T(128)S(1)} %get-tuple-element.132), channel_id=1, source_target_pairs={{0,16},{8,24},{16,32},{24,40},{32,48},{40,56},{48,64},{56,72},{64,... | collective-permute-start | bytes 1544 | tf_op jit(solution)/shard_map/ppermute | solution.py:26
  175.7 9.3 %all-to-all-start.1 = ((f32[8,1,64]{2,1,0:T(1,128)}), f32[8,1,64]{2,1,0:T(1,128)S(1)}, u32[]{:S(2)}, u32[]{:S(2)}) async-start(f32[8,1,64]{2,1,0:T(1,128)} %all_to_all.11), calls=%async_computation.1 | async-start | bytes 8192 | tf_op jit(solution)/shard_map/all_to_all | solution.py:37
  186.0 0.6 copy-start.1
where the time goes:
time: 193 us; the launch traced here: 191 us
  matrix products  102 us (53%)
  other arithmetic  43.1 us (22%)
  starting transfers between devices  26.8 us (14%)
  local copies, waits for them, and re-layouts  8.93 us (5%)
  waiting for transfers between devices  8.28 us (4%)
  loops' own time  1.96 us (1%)
    dot_general x16, matrix products, tile_terms(): jnp.einsum('kfw,w->kf', onehot_far, remote_window, precision=lax.Precisio...  27.1 us
    dot_general x16, matrix products, tile_terms(): jnp.einsum('kfw,w->kf', onehot_near, window, precision=lax.Precision.HIGH...  27 us
    dot_general x16, matrix products, tile_terms(): jnp.einsum('kfw,kf->w', onehot_far, terms, precision=lax.Precision.HIGHEST)  23.9 us
    dot_general x16, matrix products, tile_terms(): jnp.einsum('kfw,kf->w', onehot_near, terms, precision=lax.Precision.HIGHEST)  23.6 us
    select_n x16, other arithmetic, tile_terms(): weight = jnp.where(live_mask, area_tile, 0.0)  22.5 us
    ppermute x8, starting transfers between devices, from_behind(): lax.ppermute(x, axis, [(i, (i + by) % length) for i in range(length)])  16.2 us
    sub x16, other arithmetic, tile_terms(): corner_tile[:, :, None] - remote_start == remote_pos  12.8 us
    all_to_all x1, starting transfers between devices, sent_to_all(): return lax.all_to_all(copies, axis, split_axis=0, concat_axis=0, tiled=True)  5.81 us
  transfers between devices with their start and end apart: 10, of which 3 were waited for; matrix products, arithmetic and copies ran while one was open for 1% of the time, Pallas kernels for 0%

commit v1 on v0

v1 whole, which is shorter than its diff:
```python
import functools

import jax
import jax.numpy as jnp
from jax import lax
from jax.experimental import pallas as pl
from jax.experimental.pallas import tpu as pltpu
from jax.sharding import PartitionSpec as P

RADIUS = 2
OFFSETS = [k + 1 for k in range(RADIUS)] + [-(k + 1) for k in range(RADIUS)]
F32 = jnp.float32
BF16 = jnp.bfloat16
I32 = jnp.int32
NT = (((1,), (1,)), ((), ()))


def lanes_of(table, lane):
    return jnp.take_along_axis(table, lane, axis=1, mode="promise_in_bounds")


def iota(shape, dim):
    return lax.broadcasted_iota(I32, shape, dim)


def kernel(
    patches,
    subs,
    live_ref,
    heat_hbm,
    basis_hbm,
    area_hbm,
    corners_hbm,
    ssub_hbm,
    spat_hbm,
    out_ref,
    heat,
    basis,
    area,
    corners,
    ssub,
    spat,
    lists,
    ctile,
    btile,
    blast,
    rows,
    near,
    fwd_send,
    fwd_sub,
    fwd_pat,
    ret_send,
    ret_sub,
    ret_pat,
    in_sem,
    send_sem,
    recv_sem,
):
    p = lax.axis_index("patch")
    s = lax.axis_index("sub")
    owned = 8192

    cp_heat = pltpu.make_async_copy(heat_hbm, heat.at[pl.ds(8, 64)], in_sem.at[0])
    cp_ssub = pltpu.make_async_copy(ssub_hbm, ssub, in_sem.at[1])
    cp_spat = pltpu.make_async_copy(spat_hbm, spat, in_sem.at[2])
    cp_corners = pltpu.make_async_copy(corners_hbm, corners, in_sem.at[3])
    cp_basis = pltpu.make_async_copy(basis_hbm, basis, in_sem.at[4])
    cp_area = pltpu.make_async_copy(area_hbm, area, in_sem.at[5])
    copies = (cp_heat, cp_ssub, cp_spat, cp_corners, cp_basis, cp_area)
    for copy in copies:
        copy.start()

    def peer_sub(d):
        return {"patch": p, "sub": lax.rem(s + d, subs)}

    def peer_pat(offset):
        return {"patch": lax.rem(p + offset + patches, patches), "sub": s}

    barrier = pltpu.get_barrier_semaphore()
    for d in range(1, subs):
        pl.semaphore_signal(barrier, inc=1, device_id=peer_sub(d), device_id_type=pl.DeviceIdType.MESH)
    for offset in OFFSETS:
        pl.semaphore_signal(barrier, inc=1, device_id=peer_pat(offset), device_id_type=pl.DeviceIdType.MESH)

    heat[0:8, :] = jnp.zeros((8, 128), F32)
    heat[72:80, :] = jnp.zeros((8, 128), F32)
    for r in range(4):
        near[r, 0:8, :] = jnp.zeros((8, 128), F32)
        near[r, 264:272, :] = jnp.zeros((8, 128), F32)

    cp_heat.wait()
    cp_ssub.wait()
    cp_spat.wait()

    lists[0:4, :] = spat[...]
    one = ssub[...]
    lists[4:5, :] = jnp.concatenate([one, one], axis=1)
    sub8 = iota((8, 128), 0)
    picked = []
    for j in range(5):
        index = jnp.broadcast_to(lists[j : j + 1, :], (8, 128))
        lane = index & 127
        row = index >> 7
        total = jnp.zeros((8, 128), F32)
        for g in range(8):
            values = lanes_of(heat[8 + 8 * g : 16 + 8 * g, :], lane)
            total = jnp.where(row == sub8 + 8 * g, values, total)
        value = jnp.sum(total, axis=0, keepdims=True)
        fwd_send[j] = value
        picked.append(value)

    pl.semaphore_wait(barrier, subs - 1 + 2 * RADIUS)

    forward = []
    for j, offset in enumerate(OFFSETS):
        copy = pltpu.make_async_remote_copy(
            src_ref=fwd_send.at[j],
            dst_ref=fwd_pat.at[j],
            send_sem=send_sem.at[j],
            recv_sem=recv_sem.at[j],
            device_id=peer_pat(offset),
            device_id_type=pl.DeviceIdType.MESH,
        )
        copy.start()
        forward.append(copy)
    for d in range(1, subs):
        copy = pltpu.make_async_remote_copy(
            src_ref=fwd_send.at[4],
            dst_ref=fwd_sub.at[s],
            send_sem=send_sem.at[4 + d],
            recv_sem=recv_sem.at[4 + d],
            device_id=peer_sub(d),
            device_id_type=pl.DeviceIdType.MESH,
        )
        copy.start()
        forward.append(copy)
    fwd_sub[s] = picked[4]

    cp_corners.wait()
    cp_basis.wait()
    cp_area.wait()
    def relayout(j, carry):
        for r in range(4):
            col = pl.multiple_of(j * 512 + 128 * r, 128)
            row = pl.multiple_of(j * 8, 8)
            ctile[r, pl.ds(row, 3), :] = corners[:, pl.ds(col, 128)]
            block = basis[:, pl.ds(col, 128)].astype(F32)
            btile[r, pl.ds(row, 8), :] = block[0:8]
            blast[r, pl.ds(row, 1), :] = block[8:9]
        return carry

    lax.fori_loop(0, 32, relayout, 0)

    low64 = iota((8, 128), 1) < 64
    lane8 = iota((8, 128), 1)
    a16 = iota((16, 128), 0)
    b32 = iota((32, 128), 0)
    live = live_ref[0]

    def one_class(r, far0, far1):
        def one_group(g, far_sum):
            base = pl.multiple_of(g * 64, 64)
            first = 8 + 16 * g
            if r == 0:
                tab_a = heat[pl.ds(first - 1, 8, stride=2), :]
                tab_b = heat[pl.ds(first, 8, stride=2), :]
            elif r == 1:
                tab_a = jnp.where(low64, heat[pl.ds(first + 1, 8, stride=2), :], heat[pl.ds(first - 1, 8, stride=2), :])
                tab_b = heat[pl.ds(first, 8, stride=2), :]
            elif r == 2:
                tab_a = heat[pl.ds(first, 8, stride=2), :]
                tab_b = heat[pl.ds(first + 1, 8, stride=2), :]
            else:
                tab_a = jnp.where(low64, heat[pl.ds(first + 2, 8, stride=2), :], heat[pl.ds(first, 8, stride=2), :])
                tab_b = heat[pl.ds(first + 1, 8, stride=2), :]
            values = []
            for k in range(3):
                corner = ctile[r, pl.ds(base + k, 8, stride=8), :]
                lane = corner & 127
                odd = (corner >> 7) & 1
                is_far = corner >= owned
                owned_value = jnp.where(odd == (r >> 1), lanes_of(tab_b, lane), lanes_of(tab_a, lane))
                far_value = jnp.where(odd == 1, lanes_of(far1, lane), lanes_of(far0, lane))
                values.append(jnp.where(is_far, far_value, owned_value))
                start = jnp.where(is_far, 248 + 8 * r, sub8 * 8 + (64 * g + 2 * r - 4))
                rows[0, k] = ((corner >> 5) - start).astype(F32)
                rows[1, k] = (corner & 31).astype(F32)
            bas = [btile[r, pl.ds(base + i, 8, stride=8), :] for i in range(8)]
            bas.append(blast[r, pl.ds(base, 8, stride=8), :])
            grad = [bas[c] * values[0] + bas[3 + c] * values[1] + bas[6 + c] * values[2] for c in range(3)]
            length = jnp.sqrt(grad[0] * grad[0] + grad[1] * grad[1] + grad[2] * grad[2])
            slot = sub8 * 512 + lane8 + (4096 * g + 128 * r)
            weight = jnp.where(slot < live, area[pl.ds(32 * g + r, 8, stride=4), :], 0.0)
            scale = -weight / jnp.maximum(length, 1.0)
            for k in range(3):
                term = (bas[3 * k] * grad[0] + bas[3 * k + 1] * grad[1] + bas[3 * k + 2] * grad[2]) * scale
                high = term.astype(BF16).astype(F32)
                rows[2, k] = high
                rows[3, k] = term - high
            for i in range(8):
                left, right = [], []
                for k in range(3):
                    hit = jnp.broadcast_to(rows[0, k, i : i + 1, :], (16, 128)) == a16.astype(F32)
                    high = jnp.where(hit, jnp.broadcast_to(rows[2, k, i : i + 1, :], (16, 128)), 0.0)
                    low = jnp.where(hit, jnp.broadcast_to(rows[3, k, i : i + 1, :], (16, 128)), 0.0)
                    left.append(jnp.concatenate([high, low], axis=0).astype(BF16))
                    hit = jnp.broadcast_to(rows[1, k, i : i + 1, :], (32, 128)) == b32.astype(F32)
                    right.append(jnp.where(hit, 1.0, 0.0).astype(BF16))
                sums = lax.dot_general(
                    jnp.concatenate(left, axis=1), jnp.concatenate(right, axis=1), NT, preferred_element_type=F32
                )
                sums = sums[0:16] + sums[16:32]
                near[r, pl.ds(pl.multiple_of(8 + base + 8 * i, 8), 8), 0:32] = sums[0:8]
                far_sum = far_sum + sums[8:16]
            return far_sum

        return lax.fori_loop(0, 4, one_group, jnp.zeros((8, 32), F32))

    def to_rows(far_sum):
        wide = jnp.concatenate([far_sum, jnp.zeros((8, 96), F32)], axis=1)
        total = jnp.where((sub8 & 3) == 0, wide, 0.0)
        for w in range(1, 4):
            total = jnp.where((sub8 & 3) == w, pltpu.roll(wide, 32 * w, axis=1), total)
        return jnp.sum(total[0:4], axis=0, keepdims=True), jnp.sum(total[4:8], axis=0, keepdims=True)

    def wide_rows(row):
        return jnp.broadcast_to(row, (8, 128))

    for copy in forward[4:]:
        copy.wait()
    low_row = iota((1, 128), 1) < 64
    for r in range(2):
        far = []
        for q in range(2):
            far.append(wide_rows(jnp.where(low_row, fwd_sub[4 * r + 2 * q], fwd_sub[4 * r + 2 * q + 1])))
        top, bottom = to_rows(one_class(r, far[0], far[1]))
        ret_send[2 * r] = top
        ret_send[2 * r + 1] = bottom

    back = []
    for d in range(1, subs):
        to = lax.rem(s + d, subs)
        copy = pltpu.make_async_remote_copy(
            src_ref=ret_send.at[to // 2],
            dst_ref=ret_sub.at[s],
            send_sem=send_sem.at[16 + 4 + d],
            recv_sem=recv_sem.at[16 + 4 + d],
            device_id=peer_sub(d),
            device_id_type=pl.DeviceIdType.MESH,
        )
        copy.start()
        back.append(copy)
    ret_sub[s] = ret_send[s // 2]

    back_pat = []
    for r in range(2, 4):
        far = []
        for q in range(2):
            j = 2 * (r - 2) + q
            forward[j].wait()
            far.append(wide_rows(fwd_pat[j]))
        for q, row in enumerate(to_rows(one_class(r, far[0], far[1]))):
            j = 2 * (r - 2) + q
            ret_send[2 * r + q] = row
            copy = pltpu.make_async_remote_copy(
                src_ref=ret_send.at[2 * r + q],
                dst_ref=ret_pat.at[j],
                send_sem=send_sem.at[16 + j],
                recv_sem=recv_sem.at[16 + j],
                device_id=peer_pat(-OFFSETS[j]),
                device_id_type=pl.DeviceIdType.MESH,
            )
            copy.start()
            back_pat.append(copy)

    quarter = lane8 >> 5
    blocks = []
    for m in range(8):
        block = None
        for w in range(4):
            part = None
            for r in range(4):
                piece = near[r, pl.ds(32 * m + w + 12 - 2 * r, 8, stride=4), :]
                part = piece if part is None else part + piece
            if w:
                part = pltpu.roll(part, 32 * w, axis=1)
                block = jnp.where(quarter == w, part, block)
            else:
                block = part
        blocks.append(block)
    owned_sums = jnp.concatenate(blocks, axis=0)

    lane_hit, row_hit = [], []
    for j in range(5):
        index = lists[j : j + 1, :]
        lane_hit.append(jnp.where(jnp.broadcast_to(index & 127, (128, 128)) == iota((128, 128), 0), 1.0, 0.0).astype(BF16))
        row_hit.append(jnp.broadcast_to(index >> 7, (64, 128)) == iota((64, 128), 0))

    for copy in back:
        copy.wait()
    returned = None
    for s2 in range(subs):
        returned = ret_sub[s2] if returned is None else returned + ret_sub[s2]
    half = iota((1, 128), 1) >> 6
    returned = jnp.where(half == lax.rem(s, 2), returned, 0.0)
    for copy in back_pat:
        copy.wait()
    incoming = [ret_pat[j] for j in range(4)] + [returned]
    left = []
    for j in range(5):
        high = incoming[j].astype(BF16).astype(F32)
        low = incoming[j] - high
        left.append(
            jnp.concatenate(
                [
                    jnp.where(row_hit[j], jnp.broadcast_to(high, (64, 128)), 0.0),
                    jnp.where(row_hit[j], jnp.broadcast_to(low, (64, 128)), 0.0),
                ],
                axis=0,
            ).astype(BF16)
        )
    sums = lax.dot_general(
        jnp.concatenate(left, axis=1), jnp.concatenate(lane_hit, axis=1), NT, preferred_element_type=F32
    )
    out_ref[...] = owned_sums + (sums[0:64] + sums[64:128])


def per_device(patches, subs, heat, basis, area, corners, send_sub, send_pat, live_faces):
    hbm = pl.BlockSpec(memory_space=pl.ANY)
    out = pl.pallas_call(
        functools.partial(kernel, patches, subs),
        out_shape=jax.ShapeDtypeStruct((64, 128), F32),
        in_specs=[pl.BlockSpec(memory_space=pltpu.SMEM)] + [hbm] * 6,
        out_specs=pl.BlockSpec(memory_space=pltpu.VMEM),
        scratch_shapes=[
            pltpu.VMEM((80, 128), F32),
            pltpu.VMEM((9, 16384), BF16),
            pltpu.VMEM((128, 128), F32),
            pltpu.VMEM((3, 16384), I32),
            pltpu.VMEM((1, 64), I32),
            pltpu.VMEM((4, 128), I32),
            pltpu.VMEM((8, 128), I32),
            pltpu.VMEM((4, 256, 128), I32),
            pltpu.VMEM((4, 256, 128), F32),
            pltpu.VMEM((4, 256, 128), F32),
            pltpu.VMEM((4, 3, 8, 128), F32),
            pltpu.VMEM((4, 272, 128), F32),
            pltpu.VMEM((5, 1, 128), F32),
            pltpu.VMEM((8, 1, 128), F32),
            pltpu.VMEM((4, 1, 128), F32),
            pltpu.VMEM((8, 1, 128), F32),
            pltpu.VMEM((8, 1, 128), F32),
            pltpu.VMEM((4, 1, 128), F32),
            pltpu.SemaphoreType.DMA((6,)),
            pltpu.SemaphoreType.DMA((32,)),
            pltpu.SemaphoreType.DMA((32,)),
        ],
        compiler_params=pltpu.CompilerParams(collective_id=0, has_side_effects=True),
        name="divergence",
    )(
        live_faces,
        heat.reshape(64, 128),
        basis,
        area.reshape(128, 128),
        corners,
        send_sub.reshape(1, 64),
        send_pat,
    )
    return out.reshape(-1)


def solution(mesh):
    placed = (
        P(("patch", "sub")),
        P(None, ("patch", "sub")),
        P(("patch", "sub")),
        P(None, ("patch", "sub")),
        P(("patch", "sub")),
        P(None, ("patch", "sub")),
        P(("patch", "sub")),
    )
    return jax.shard_map(
        functools.partial(per_device, mesh.shape["patch"], mesh.shape["sub"]),
        mesh=mesh,
        in_specs=placed,
        out_specs=P(("patch", "sub")),
        check_vma=False,
    )
```

time: 193 us -> 25.5 us (0.13); the launches traced: 191 us -> 25.4 us
  matrix products: 102 us -> 0 us
  other arithmetic: 43.1 us -> 0 us
  starting transfers between devices: 26.8 us -> 0 us
  Pallas kernels: 0 us -> 23.3 us
  waiting for transfers between devices: 8.28 us -> 0 us
  local copies, waits for them, and re-layouts: 8.93 us -> 1.38 us
  loops' own time: 1.96 us -> 0 us
    dot_general x64 -> x0, matrix products: 102 us -> none  [the longest x16 27.1 us: tile_terms(): jnp.einsum('kfw,w->kf', onehot_far, remote_window, precision=lax.Precisio...]
    pallas_call x0 -> x1, Pallas kernels: none -> 23.3 us  [per_device(): pl.pallas_call(functools.partial(kernel, patches, subs), out_shape=jax.Sh...]
    select_n x20 -> x0, other arithmetic: 22.5 us -> none  [the longest x16 22.5 us: tile_terms(): weight = jnp.where(live_mask, area_tile, 0.0)]
    ppermute x8 -> x0, starting transfers between devices: 16.2 us -> none  [from_behind(): lax.ppermute(x, axis, [(i, (i + by) % length) for i in range(length)])]
    sub x16 -> x0, other arithmetic: 12.8 us -> none  [tile_terms(): corner_tile[:, :, None] - remote_start == remote_pos]
    all_to_all x2 -> x0, starting transfers between devices: 10.6 us -> none  [the longest x1 5.81 us: sent_to_all(): return lax.all_to_all(copies, axis, split_axis=0, concat_axis=0, tiled=True)]
    all_to_all x2 -> x0, waiting for transfers between devices: 7.18 us -> none  [the longest x1 3.74 us: sent_to_all(): return lax.all_to_all(copies, axis, split_axis=0, concat_axis=0, tiled=True)]
    scatter-add x2 -> x0, other arithmetic: 5.31 us -> none  [the longest x1 4.35 us: per_device(): result = result.at[send_pat.reshape(-1)].add(returned.reshape(-1))]
  transfers between devices with their start and end apart: 10 -> 0, of which waited for: 3 -> 0; matrix products, arithmetic and copies ran while one was open for 1% -> 0% of each run, Pallas kernels for 0% -> 0%
where the time goes in v1:
time: 25.5 us; the launch traced here: 25.4 us
  Pallas kernels  23.3 us (91%)
  local copies, waits for them, and re-layouts  1.38 us (5%)
  between operations  0.66 us (3%)
    pallas_call x1, Pallas kernels, per_device(): pl.pallas_call(functools.partial(kernel, patches, subs), out_shape=jax.Sh...  23.3 us
    unnamed x1, local copies, waits for them, and re-layouts  1.38 us

profile of v1, /device:TPU:1, one launch (start us, length us, event | category | flops | bytes accessed | tf_op | source)
XLA Modules:
  0.0 25.4 jit_solution(1439979660689188174)
XLA Ops:
  0.7 23.3 %divergence.1 = f32[64,128]{1,0:T(8,128)} custom-call(s32[1]{0:T(128)S(6)} %copy.9.live_ref, f32[64,128]{1,0:T(8,128)} %bitcast.6, bf16[9,16384]{1,0:T(8,128)(2,1)} %basis_hbm.1, f32[128,128]{1,0:T(8,128)} %bitcast.5, s32[3,16384]{1,0:T(4,128)} %corners_hbm.1, s32[1,64]{1,0:T(1,128)} %bitcast.7, s32[4,128]{1,0:T(4,128)} %spat_hbm.1), custom_call_target="tpu_custom_call" | custom-call | tf_op jit(solution)/shard_map/divergence/pallas_call | solution.py:330
  24.0 1.4 %copy.10 = f32[8192]{0:T(1024)} copy(f32[8192]{0:T(1024)} %bitcast.4) | data formatting | bytes 65536

commit v2 on v1

--- a/solution.py
+++ b/solution.py
@@ -26,7 +26,7 @@
 def kernel(
     patches,
     subs,
-    live_ref,
+    live_hbm,
     heat_hbm,
     basis_hbm,
     area_hbm,
@@ -34,6 +34,7 @@
     ssub_hbm,
     spat_hbm,
     out_ref,
+    live_ref,
     heat,
     basis,
     area,
@@ -44,6 +45,10 @@
     ctile,
     btile,
     blast,
+    cgrp,
+    vgrp,
+    bgrp,
+    wgrp,
     rows,
     near,
     fwd_send,
@@ -60,27 +65,28 @@
     s = lax.axis_index("sub")
     owned = 8192
 
+    def peer_sub(d):
+        return {"patch": p, "sub": lax.rem(s + d, subs)}
+
+    def peer_pat(offset):
+        return {"patch": lax.rem(p + offset + patches, patches), "sub": s}
+
+    barrier = pltpu.get_barrier_semaphore()
+    for offset in OFFSETS:
+        pl.semaphore_signal(barrier, inc=1, device_id=peer_pat(offset), device_id_type=pl.DeviceIdType.MESH)
+    for d in range(1, subs):
+        pl.semaphore_signal(barrier, inc=1, device_id=peer_sub(d), device_id_type=pl.DeviceIdType.MESH)
+
     cp_heat = pltpu.make_async_copy(heat_hbm, heat.at[pl.ds(8, 64)], in_sem.at[0])
     cp_ssub = pltpu.make_async_copy(ssub_hbm, ssub, in_sem.at[1])
     cp_spat = pltpu.make_async_copy(spat_hbm, spat, in_sem.at[2])
     cp_corners = pltpu.make_async_copy(corners_hbm, corners, in_sem.at[3])
     cp_basis = pltpu.make_async_copy(basis_hbm, basis, in_sem.at[4])
     cp_area = pltpu.make_async_copy(area_hbm, area, in_sem.at[5])
-    copies = (cp_heat, cp_ssub, cp_spat, cp_corners, cp_basis, cp_area)
+    cp_live = pltpu.make_async_copy(live_hbm, live_ref, in_sem.at[6])
+    copies = (cp_heat, cp_ssub, cp_spat, cp_corners, cp_basis, cp_area, cp_live)
     for copy in copies:
         copy.start()
-
-    def peer_sub(d):
-        return {"patch": p, "sub": lax.rem(s + d, subs)}
-
-    def peer_pat(offset):
-        return {"patch": lax.rem(p + offset + patches, patches), "sub": s}
-
-    barrier = pltpu.get_barrier_semaphore()
-    for d in range(1, subs):
-        pl.semaphore_signal(barrier, inc=1, device_id=peer_sub(d), device_id_type=pl.DeviceIdType.MESH)
-    for offset in OFFSETS:
-        pl.semaphore_signal(barrier, inc=1, device_id=peer_pat(offset), device_id_type=pl.DeviceIdType.MESH)
 
     heat[0:8, :] = jnp.zeros((8, 128), F32)
     heat[72:80, :] = jnp.zeros((8, 128), F32)
@@ -139,6 +145,8 @@
     cp_corners.wait()
     cp_basis.wait()
     cp_area.wait()
+    cp_live.wait()
+
     def relayout(j, carry):
         for r in range(4):
             col = pl.multiple_of(j * 512 + 128 * r, 128)
@@ -153,68 +161,73 @@
 
     low64 = iota((8, 128), 1) < 64
     lane8 = iota((8, 128), 1)
-    a16 = iota((16, 128), 0)
-    b32 = iota((32, 128), 0)
+    a16 = iota((16, 128), 0).astype(F32)
+    b32 = iota((32, 128), 0).astype(F32)
     live = live_ref[0]
 
-    def one_class(r, far0, far1):
-        def one_group(g, far_sum):
-            base = pl.multiple_of(g * 64, 64)
-            first = 8 + 16 * g
-            if r == 0:
-                tab_a = heat[pl.ds(first - 1, 8, stride=2), :]
-                tab_b = heat[pl.ds(first, 8, stride=2), :]
-            elif r == 1:
-                tab_a = jnp.where(low64, heat[pl.ds(first + 1, 8, stride=2), :], heat[pl.ds(first - 1, 8, stride=2), :])
-                tab_b = heat[pl.ds(first, 8, stride=2), :]
-            elif r == 2:
-                tab_a = heat[pl.ds(first, 8, stride=2), :]
-                tab_b = heat[pl.ds(first + 1, 8, stride=2), :]
-            else:
-                tab_a = jnp.where(low64, heat[pl.ds(first + 2, 8, stride=2), :], heat[pl.ds(first, 8, stride=2), :])
-                tab_b = heat[pl.ds(first + 1, 8, stride=2), :]
-            values = []
+    def prepare(g, carry):
+        base = pl.multiple_of(g * 64, 64)
+        first = 8 + 16 * g
+        for r in range(4):
+            m = first + (r >> 1)
+            tab_a = heat[pl.ds(m - 1, 8, stride=2), :]
+            tab_b = heat[pl.ds(m, 8, stride=2), :]
+            if r & 1:
+                tab_a = jnp.where(low64, heat[pl.ds(m + 1, 8, stride=2), :], tab_a)
             for k in range(3):
                 corner = ctile[r, pl.ds(base + k, 8, stride=8), :]
                 lane = corner & 127
                 odd = (corner >> 7) & 1
-                is_far = corner >= owned
-                owned_value = jnp.where(odd == (r >> 1), lanes_of(tab_b, lane), lanes_of(tab_a, lane))
-                far_value = jnp.where(odd == 1, lanes_of(far1, lane), lanes_of(far0, lane))
-                values.append(jnp.where(is_far, far_value, owned_value))
-                start = jnp.where(is_far, 248 + 8 * r, sub8 * 8 + (64 * g + 2 * r - 4))
-                rows[0, k] = ((corner >> 5) - start).astype(F32)
-                rows[1, k] = (corner & 31).astype(F32)
-            bas = [btile[r, pl.ds(base + i, 8, stride=8), :] for i in range(8)]
-            bas.append(blast[r, pl.ds(base, 8, stride=8), :])
+                cgrp[r, g, k] = corner
+                vgrp[r, g, k] = jnp.where(odd == (r >> 1), lanes_of(tab_b, lane), lanes_of(tab_a, lane))
+                start = jnp.where(corner >= owned, 248 + 8 * r, sub8 * 8 + (64 * g + 2 * r - 4))
+                rows[r, g, 0, k] = ((corner >> 5) - start).astype(F32)
+                rows[r, g, 1, k] = (corner & 31).astype(F32)
+            for i in range(8):
+                bgrp[r, g, i] = btile[r, pl.ds(base + i, 8, stride=8), :]
+            bgrp[r, g, 8] = blast[r, pl.ds(base, 8, stride=8), :]
+            slot = sub8 * 512 + lane8 + (4096 * g + 128 * r)
+            wgrp[r, g] = jnp.where(slot < live, area[pl.ds(32 * g + r, 8, stride=4), :], 0.0)
+        return carry
+
+    lax.fori_loop(0, 4, prepare, 0)
+
+    def one_class(r, far0, far1):
+        for g in range(4):
+            values = []
+            for k in range(3):
+                corner = cgrp[r, g, k]
+                lane = corner & 127
+                far_value = jnp.where(((corner >> 7) & 1) == 1, lanes_of(far1, lane), lanes_of(far0, lane))
+                values.append(jnp.where(corner >= owned, far_value, vgrp[r, g, k]))
+            bas = [bgrp[r, g, i] for i in range(9)]
             grad = [bas[c] * values[0] + bas[3 + c] * values[1] + bas[6 + c] * values[2] for c in range(3)]
             length = jnp.sqrt(grad[0] * grad[0] + grad[1] * grad[1] + grad[2] * grad[2])
-            slot = sub8 * 512 + lane8 + (4096 * g + 128 * r)
-            weight = jnp.where(slot < live, area[pl.ds(32 * g + r, 8, stride=4), :], 0.0)
-            scale = -weight / jnp.maximum(length, 1.0)
+            scale = -wgrp[r, g] / jnp.maximum(length, 1.0)
             for k in range(3):
                 term = (bas[3 * k] * grad[0] + bas[3 * k + 1] * grad[1] + bas[3 * k + 2] * grad[2]) * scale
                 high = term.astype(BF16).astype(F32)
-                rows[2, k] = high
-                rows[3, k] = term - high
+                rows[r, g, 2, k] = high
+                rows[r, g, 3, k] = term - high
+        far_sum = jnp.zeros((8, 32), F32)
+        for g in range(4):
             for i in range(8):
                 left, right = [], []
                 for k in range(3):
-                    hit = jnp.broadcast_to(rows[0, k, i : i + 1, :], (16, 128)) == a16.astype(F32)
-                    high = jnp.where(hit, jnp.broadcast_to(rows[2, k, i : i + 1, :], (16, 128)), 0.0)
-                    low = jnp.where(hit, jnp.broadcast_to(rows[3, k, i : i + 1, :], (16, 128)), 0.0)
+                    a_row, b_row, high, low = (rows[r, g, q, k, i : i + 1, :] for q in range(4))
+                    hit = jnp.broadcast_to(a_row, (16, 128)) == a16
+                    high = jnp.where(hit, jnp.broadcast_to(high, (16, 128)), 0.0)
+                    low = jnp.where(hit, jnp.broadcast_to(low, (16, 128)), 0.0)
                     left.append(jnp.concatenate([high, low], axis=0).astype(BF16))
-                    hit = jnp.broadcast_to(rows[1, k, i : i + 1, :], (32, 128)) == b32.astype(F32)
+                    hit = jnp.broadcast_to(b_row, (32, 128)) == b32
                     right.append(jnp.where(hit, 1.0, 0.0).astype(BF16))
                 sums = lax.dot_general(
                     jnp.concatenate(left, axis=1), jnp.concatenate(right, axis=1), NT, preferred_element_type=F32
                 )
                 sums = sums[0:16] + sums[16:32]
-                near[r, pl.ds(pl.multiple_of(8 + base + 8 * i, 8), 8), 0:32] = sums[0:8]
+                near[r, pl.ds(8 + 64 * g + 8 * i, 8), 0:32] = sums[0:8]
                 far_sum = far_sum + sums[8:16]
-            return far_sum
-
-        return lax.fori_loop(0, 4, one_group, jnp.zeros((8, 32), F32))
+        return far_sum
 
     def to_rows(far_sum):
         wide = jnp.concatenate([far_sum, jnp.zeros((8, 96), F32)], axis=1)
@@ -226,39 +239,13 @@
     def wide_rows(row):
         return jnp.broadcast_to(row, (8, 128))
 
-    for copy in forward[4:]:
-        copy.wait()
-    low_row = iota((1, 128), 1) < 64
-    for r in range(2):
+    back, back_pat = [], []
+
+    def patch_class(r):
         far = []
         for q in range(2):
-            far.append(wide_rows(jnp.where(low_row, fwd_sub[4 * r + 2 * q], fwd_sub[4 * r + 2 * q + 1])))
-        top, bottom = to_rows(one_class(r, far[0], far[1]))
-        ret_send[2 * r] = top
-        ret_send[2 * r + 1] = bottom
-
-    back = []
-    for d in range(1, subs):
-        to = lax.rem(s + d, subs)
-        copy = pltpu.make_async_remote_copy(
-            src_ref=ret_send.at[to // 2],
-            dst_ref=ret_sub.at[s],
-            send_sem=send_sem.at[16 + 4 + d],
-            recv_sem=recv_sem.at[16 + 4 + d],
-            device_id=peer_sub(d),
-            device_id_type=pl.DeviceIdType.MESH,
-        )
-        copy.start()
-        back.append(copy)
-    ret_sub[s] = ret_send[s // 2]
-
-    back_pat = []
-    for r in range(2, 4):
-        far = []
-        for q in range(2):
-            j = 2 * (r - 2) + q
-            forward[j].wait()
-            far.append(wide_rows(fwd_pat[j]))
+            forward[2 * (r - 2) + q].wait()
+            far.append(wide_rows(fwd_pat[2 * (r - 2) + q]))
         for q, row in enumerate(to_rows(one_class(r, far[0], far[1]))):
             j = 2 * (r - 2) + q
             ret_send[2 * r + q] = row
@@ -272,6 +259,35 @@
             )
             copy.start()
             back_pat.append(copy)
+
+    def group_classes():
+        low_row = iota((1, 128), 1) < 64
+        for copy in forward[4:]:
+            copy.wait()
+        for r in range(2):
+            far = []
+            for q in range(2):
+                far.append(wide_rows(jnp.where(low_row, fwd_sub[4 * r + 2 * q], fwd_sub[4 * r + 2 * q + 1])))
+            top, bottom = to_rows(one_class(r, far[0], far[1]))
+            ret_send[2 * r] = top
+            ret_send[2 * r + 1] = bottom
+        for d in range(1, subs):
+            to = lax.rem(s + d, subs)
+            copy = pltpu.make_async_remote_copy(
+                src_ref=ret_send.at[to // 2],
+                dst_ref=ret_sub.at[s],
+                send_sem=send_sem.at[16 + 4 + d],
+                recv_sem=recv_sem.at[16 + 4 + d],
+                device_id=peer_sub(d),
+                device_id_type=pl.DeviceIdType.MESH,
+            )
+            copy.start()
+            back.append(copy)
+        ret_sub[s] = ret_send[s // 2]
+
+    patch_class(3)
+    group_classes()
+    patch_class(2)
 
     quarter = lane8 >> 5
     blocks = []
@@ -329,10 +345,11 @@
     hbm = pl.BlockSpec(memory_space=pl.ANY)
     out = pl.pallas_call(
         functools.partial(kernel, patches, subs),
-        out_shape=jax.ShapeDtypeStruct((64, 128), F32),
-        in_specs=[pl.BlockSpec(memory_space=pltpu.SMEM)] + [hbm] * 6,
+        out_shape=pltpu.VMEM((64, 128), F32),
+        in_specs=[hbm] * 7,
         out_specs=pl.BlockSpec(memory_space=pltpu.VMEM),
         scratch_shapes=[
+            pltpu.SMEM((1,), I32),
             pltpu.VMEM((80, 128), F32),
             pltpu.VMEM((9, 16384), BF16),
             pltpu.VMEM((128, 128), F32),
@@ -343,7 +360,11 @@
             pltpu.VMEM((4, 256, 128), I32),
             pltpu.VMEM((4, 256, 128), F32),
             pltpu.VMEM((4, 256, 128), F32),
-            pltpu.VMEM((4, 3, 8, 128), F32),
+            pltpu.VMEM((4, 4, 3, 8, 128), I32),
+            pltpu.VMEM((4, 4, 3, 8, 128), F32),
+            pltpu.VMEM((4, 4, 9, 8, 128), F32),
+            pltpu.VMEM((4, 4, 8, 128), F32),
+            pltpu.VMEM((4, 4, 4, 3, 8, 128), F32),
             pltpu.VMEM((4, 272, 128), F32),
             pltpu.VMEM((5, 1, 128), F32),
             pltpu.VMEM((8, 1, 128), F32),
@@ -351,20 +372,27 @@
             pltpu.VMEM((8, 1, 128), F32),
             pltpu.VMEM((8, 1, 128), F32),
             pltpu.VMEM((4, 1, 128), F32),
-            pltpu.SemaphoreType.DMA((6,)),
+            pltpu.SemaphoreType.DMA((7,)),
             pltpu.SemaphoreType.DMA((32,)),
             pltpu.SemaphoreType.DMA((32,)),
         ],
-        compiler_params=pltpu.CompilerParams(collective_id=0, has_side_effects=True),
+        compiler_params=pltpu.CompilerParams(
+            collective_id=0, has_side_effects=True, vmem_limit_bytes=32 * 1024 * 1024
+        ),
         name="divergence",
     )(
         live_faces,
-        heat.reshape(64, 128),
-        basis,
-        area.reshape(128, 128),
-        corners,
-        send_sub.reshape(1, 64),
-        send_pat,
+        *(
+            pltpu.with_memory_space_constraint(x, pltpu.HBM)
+            for x in (
+                heat.reshape(64, 128),
+                basis,
+                area.reshape(128, 128),
+                corners,
+                send_sub.reshape(1, 64),
+                send_pat,
+            )
+        )
     )
     return out.reshape(-1)
 

time: 25.5 us -> 21.1 us (0.83)
  the two profiles are of different devices: /device:TPU:1 before, /device:TPU:2 now
where the time goes in v2:
time: 21.1 us; the launch traced here: 21 us
  Pallas kernels  19.7 us (93%)
  between operations  0.66 us (3%)
  local copies, waits for them, and re-layouts  0.62 us (3%)
    pallas_call x1, Pallas kernels, per_device(): pl.pallas_call(functools.partial(kernel, patches, subs), out_shape=pltpu....  19.7 us
    unnamed x1, local copies, waits for them, and re-layouts  0.62 us

profile of v2, /device:TPU:2, one launch (start us, length us, event | category | flops | bytes accessed | tf_op | source)
XLA Modules:
  0.0 21.0 jit_solution(11216456683760463463)
XLA Ops:
  0.7 19.7 %divergence.1 = f32[64,128]{1,0:T(8,128)S(1)} custom-call(s32[1]{0:T(128)S(6)} %copy.10.live_hbm, f32[64,128]{1,0:T(8,128)} %bitcast.6, bf16[9,16384]{1,0:T(8,128)(2,1)} %basis_hbm.1, f32[128,128]{1,0:T(8,128)} %bitcast.5, s32[3,16384]{1,0:T(4,128)} %corners_hbm.1, s32[1,64]{1,0:T(1,128)} %bitcast.7, s32[4,128]{1,0:T(4,128)} %spat_hbm.1), custom_call_target="tpu_custom_call" | custom-call | tf_op jit(solution)/shard_map/divergence/pallas_call | solution.py:346
  20.4 0.6 %copy.9 = f32[8192]{0:T(1024)} copy(f32[8192]{0:T(1024)S(1)} %bitcast.4) | data formatting | bytes 65536

commit v3 on v2

--- a/solution.py
+++ b/solution.py
@@ -13,6 +13,7 @@
 BF16 = jnp.bfloat16
 I32 = jnp.int32
 NT = (((1,), (1,)), ((), ()))
+ROW = 8
 
 
 def lanes_of(table, lane):
@@ -54,6 +55,7 @@
     fwd_send,
     fwd_sub,
     fwd_pat,
+    relay,
     ret_send,
     ret_sub,
     ret_pat,
@@ -72,8 +74,24 @@
         return {"patch": lax.rem(p + offset + patches, patches), "sub": s}
 
     barrier = pltpu.get_barrier_semaphore()
+    last_row = patches - ROW
     for offset in OFFSETS:
-        pl.semaphore_signal(barrier, inc=1, device_id=peer_pat(offset), device_id_type=pl.DeviceIdType.MESH)
+        to = p + offset
+        if offset > 0:
+            to = jnp.where(to >= patches, to - ROW, to)
+        pl.semaphore_signal(
+            barrier,
+            inc=1,
+            device_id={"patch": lax.rem(to + patches, patches), "sub": s},
+            device_id_type=pl.DeviceIdType.MESH,
+        )
+
+    @pl.when((p >= last_row) & (p < last_row + RADIUS))
+    def _():
+        pl.semaphore_signal(
+            barrier, inc=1, device_id={"patch": p - last_row, "sub": s}, device_id_type=pl.DeviceIdType.MESH
+        )
+
     for d in range(1, subs):
         pl.semaphore_signal(barrier, inc=1, device_id=peer_sub(d), device_id_type=pl.DeviceIdType.MESH)
 
@@ -115,9 +133,12 @@
         fwd_send[j] = value
         picked.append(value)
 
-    pl.semaphore_wait(barrier, subs - 1 + 2 * RADIUS)
-
-    forward = []
+    signals = subs - 1 + 2 * RADIUS
+    for k in range(RADIUS):
+        signals = signals + (RADIUS - k) * (p == last_row + k).astype(I32) - (RADIUS - 1 - k) * (p == k).astype(I32)
+    pl.semaphore_wait(barrier, signals)
+
+    forward, relays = [], []
     for j, offset in enumerate(OFFSETS):
         copy = pltpu.make_async_remote_copy(
             src_ref=fwd_send.at[j],
@@ -127,8 +148,30 @@
             device_id=peer_pat(offset),
             device_id_type=pl.DeviceIdType.MESH,
         )
-        copy.start()
         forward.append(copy)
+        if offset > 0:
+            copy.start()
+            continue
+        slot = -offset - 1
+        first = pltpu.make_async_remote_copy(
+            src_ref=fwd_send.at[j],
+            dst_ref=relay.at[slot],
+            send_sem=send_sem.at[j],
+            recv_sem=recv_sem.at[12 + slot],
+            device_id=peer_pat(-ROW),
+            device_id_type=pl.DeviceIdType.MESH,
+        )
+        second = pltpu.make_async_remote_copy(
+            src_ref=relay.at[slot],
+            dst_ref=fwd_pat.at[j],
+            send_sem=send_sem.at[12 + slot],
+            recv_sem=recv_sem.at[j],
+            device_id=peer_pat(ROW + offset - patches),
+            device_id_type=pl.DeviceIdType.MESH,
+        )
+        relays.append(((p >= last_row) & (p < last_row - offset), first, second))
+        pl.when(p < -offset)(first.start)
+        pl.when(p >= -offset)(copy.start)
     for d in range(1, subs):
         copy = pltpu.make_async_remote_copy(
             src_ref=fwd_send.at[4],
@@ -140,6 +183,13 @@
         )
         copy.start()
         forward.append(copy)
+    for on, first, second in relays:
+
+        @pl.when(on)
+        def _(first=first, second=second):
+            first.wait_recv()
+            second.start()
+
     fwd_sub[s] = picked[4]
 
     cp_corners.wait()
@@ -321,6 +371,8 @@
     returned = jnp.where(half == lax.rem(s, 2), returned, 0.0)
     for copy in back_pat:
         copy.wait()
+    for on, first, second in relays:
+        pl.when(on)(second.wait_send)
     incoming = [ret_pat[j] for j in range(4)] + [returned]
     left = []
     for j in range(5):
@@ -369,6 +421,7 @@
             pltpu.VMEM((5, 1, 128), F32),
             pltpu.VMEM((8, 1, 128), F32),
             pltpu.VMEM((4, 1, 128), F32),
+            pltpu.VMEM((RADIUS, 1, 128), F32),
             pltpu.VMEM((8, 1, 128), F32),
             pltpu.VMEM((8, 1, 128), F32),
             pltpu.VMEM((4, 1, 128), F32),

time: 21.1 us -> 19.2 us (0.910)
  Pallas kernels: 19.7 us -> 17.8 us
    pallas_call x1, Pallas kernels: 19.7 us -> 17.8 us  [per_device(): pl.pallas_call(functools.partial(kernel, patches, subs), out_shape=pltpu....]
where the time goes in v3:
time: 19.2 us; the launch traced here: 19.1 us
  Pallas kernels  17.8 us (93%)
  between operations  0.66 us (3%)
  local copies, waits for them, and re-layouts  0.62 us (3%)
    pallas_call x1, Pallas kernels, per_device(): pl.pallas_call(functools.partial(kernel, patches, subs), out_shape=pltpu....  17.8 us
    unnamed x1, local copies, waits for them, and re-layouts  0.62 us

profile of v3, /device:TPU:2, one launch (start us, length us, event | category | flops | bytes accessed | tf_op | source)
XLA Modules:
  0.0 19.1 jit_solution(16003276254829447609)
XLA Ops:
  0.7 17.8 %divergence.1 = f32[64,128]{1,0:T(8,128)S(1)} custom-call(s32[1]{0:T(128)S(6)} %copy.10.live_hbm, f32[64,128]{1,0:T(8,128)} %bitcast.6, bf16[9,16384]{1,0:T(8,128)(2,1)} %basis_hbm.1, f32[128,128]{1,0:T(8,128)} %bitcast.5, s32[3,16384]{1,0:T(4,128)} %corners_hbm.1, s32[1,64]{1,0:T(1,128)} %bitcast.7, s32[4,128]{1,0:T(4,128)} %spat_hbm.1), custom_call_target="tpu_custom_call" | custom-call | tf_op jit(solution)/shard_map/divergence/pallas_call | solution.py:398
  18.5 0.6 %copy.9 = f32[8192]{0:T(1024)} copy(f32[8192]{0:T(1024)S(1)} %bitcast.4) | data formatting | bytes 65536

commit v4 on v2

--- a/solution.py
+++ b/solution.py
@@ -13,6 +13,7 @@
 BF16 = jnp.bfloat16
 I32 = jnp.int32
 NT = (((1,), (1,)), ((), ()))
+ROW = 8
 
 
 def lanes_of(table, lane):
@@ -54,6 +55,7 @@
     fwd_send,
     fwd_sub,
     fwd_pat,
+    relay,
     ret_send,
     ret_sub,
     ret_pat,
@@ -72,8 +74,32 @@
         return {"patch": lax.rem(p + offset + patches, patches), "sub": s}
 
     barrier = pltpu.get_barrier_semaphore()
+    last_row = patches - ROW
+    at = lax.rem(p, ROW)
+    odd_core = lax.rem(s, 2)
+    linked = s + 1 - odd_core
     for offset in OFFSETS:
-        pl.semaphore_signal(barrier, inc=1, device_id=peer_pat(offset), device_id_type=pl.DeviceIdType.MESH)
+        to, core = p + offset, s
+        if offset > 0:
+            to = jnp.where(to >= patches, to - ROW, to)
+            core = jnp.where(p + offset >= patches, linked, s)
+        pl.semaphore_signal(
+            barrier,
+            inc=1,
+            device_id={"patch": lax.rem(to + patches, patches), "sub": core},
+            device_id_type=pl.DeviceIdType.MESH,
+        )
+
+    @pl.when((p >= last_row) & (at < RADIUS) & (odd_core == 1))
+    def _():
+        for back_by in range(2):
+            pl.semaphore_signal(
+                barrier,
+                inc=1,
+                device_id={"patch": p - last_row, "sub": s - back_by},
+                device_id_type=pl.DeviceIdType.MESH,
+            )
+
     for d in range(1, subs):
         pl.semaphore_signal(barrier, inc=1, device_id=peer_sub(d), device_id_type=pl.DeviceIdType.MESH)
 
@@ -115,9 +141,16 @@
         fwd_send[j] = value
         picked.append(value)
 
-    pl.semaphore_wait(barrier, subs - 1 + 2 * RADIUS)
-
-    forward = []
+    signals = subs - 1 + 2 * RADIUS
+    for k in range(RADIUS):
+        over = RADIUS - k
+        here = (at == k).astype(I32)
+        first_row = (p < ROW).astype(I32)
+        signals = signals + here * first_row * (1 - over)
+        signals = signals + here * (p >= last_row).astype(I32) * odd_core * 2 * over
+    pl.semaphore_wait(barrier, signals)
+
+    forward, relays = [], []
     for j, offset in enumerate(OFFSETS):
         copy = pltpu.make_async_remote_copy(
             src_ref=fwd_send.at[j],
@@ -127,8 +160,46 @@
             device_id=peer_pat(offset),
             device_id_type=pl.DeviceIdType.MESH,
         )
-        copy.start()
         forward.append(copy)
+        if offset > 0:
+            copy.start()
+            continue
+        slot = -offset - 1
+        over, via = at < -offset, p < -offset
+        place = odd_core * RADIUS + slot
+        first = pltpu.make_async_remote_copy(
+            src_ref=fwd_send.at[j],
+            dst_ref=relay.at[place],
+            send_sem=send_sem.at[j],
+            recv_sem=recv_sem.at[32 + place],
+            device_id={"patch": lax.rem(p + last_row, patches), "sub": linked},
+            device_id_type=pl.DeviceIdType.MESH,
+        )
+        pl.when(via)(first.start)
+        pl.when(jnp.logical_not(via))(copy.start)
+        for kind in range(2):
+            on = (odd_core == 1) & over & (p >= last_row)
+            place = kind * RADIUS + slot
+            hop = {
+                "src_ref": relay.at[place],
+                "dst_ref": fwd_pat.at[j],
+                "send_sem": send_sem.at[32 + place],
+                "device_id": {
+                    "patch": lax.rem(p + ROW + offset, patches),
+                    "sub": s if kind == 1 else s - odd_core,
+                },
+                "device_id_type": pl.DeviceIdType.MESH,
+            }
+            taken = pltpu.make_async_remote_copy(**{**hop, "dst_ref": relay.at[place]}, recv_sem=recv_sem.at[32 + place])
+            onward = pltpu.make_async_remote_copy(**hop, recv_sem=recv_sem.at[j])
+            relays.append((on, taken, onward))
+    for on, taken, onward in reversed(relays):
+
+        @pl.when(on)
+        def _(taken=taken, onward=onward):
+            taken.wait_recv()
+            onward.start()
+
     for d in range(1, subs):
         copy = pltpu.make_async_remote_copy(
             src_ref=fwd_send.at[4],
@@ -161,7 +232,7 @@
 
     low64 = iota((8, 128), 1) < 64
     lane8 = iota((8, 128), 1)
-    a16 = iota((16, 128), 0).astype(F32)
+    a8 = iota((8, 128), 0).astype(F32)
     b32 = iota((32, 128), 0).astype(F32)
     live = live_ref[0]
 
@@ -192,6 +263,16 @@
 
     lax.fori_loop(0, 4, prepare, 0)
 
+    def term_rows(r, g, i, k, places):
+        hit = jnp.broadcast_to(rows[r, g, 0, k, i : i + 1, :], (8, 128)) == places
+        high = jnp.where(hit, jnp.broadcast_to(rows[r, g, 2, k, i : i + 1, :], (8, 128)), 0.0)
+        low = jnp.where(hit, jnp.broadcast_to(rows[r, g, 3, k, i : i + 1, :], (8, 128)), 0.0)
+        return jnp.concatenate([high, low], axis=0).astype(BF16)
+
+    def lane_rows(r, g, i, k):
+        hit = jnp.broadcast_to(rows[r, g, 1, k, i : i + 1, :], (32, 128)) == b32
+        return jnp.where(hit, 1.0, 0.0).astype(BF16)
+
     def one_class(r, far0, far1):
         for g in range(4):
             values = []
@@ -211,23 +292,28 @@
                 rows[r, g, 3, k] = term - high
         far_sum = jnp.zeros((8, 32), F32)
         for g in range(4):
+            left, right = [], []
             for i in range(8):
-                left, right = [], []
                 for k in range(3):
-                    a_row, b_row, high, low = (rows[r, g, q, k, i : i + 1, :] for q in range(4))
-                    hit = jnp.broadcast_to(a_row, (16, 128)) == a16
-                    high = jnp.where(hit, jnp.broadcast_to(high, (16, 128)), 0.0)
-                    low = jnp.where(hit, jnp.broadcast_to(low, (16, 128)), 0.0)
-                    left.append(jnp.concatenate([high, low], axis=0).astype(BF16))
-                    hit = jnp.broadcast_to(b_row, (32, 128)) == b32
-                    right.append(jnp.where(hit, 1.0, 0.0).astype(BF16))
+                    left.append(term_rows(r, g, i, k, a8 + 8.0))
+                    right.append(lane_rows(r, g, i, k))
+            sums = lax.dot_general(
+                jnp.concatenate(left, axis=1), jnp.concatenate(right, axis=1), NT, preferred_element_type=F32
+            )
+            far_sum = far_sum + (sums[0:8] + sums[8:16])
+        return far_sum
+
+    def near_group(g, carry):
+        for r in range(4):
+            for i in range(8):
                 sums = lax.dot_general(
-                    jnp.concatenate(left, axis=1), jnp.concatenate(right, axis=1), NT, preferred_element_type=F32
+                    jnp.concatenate([term_rows(r, g, i, k, a8) for k in range(3)], axis=1),
+                    jnp.concatenate([lane_rows(r, g, i, k) for k in range(3)], axis=1),
+                    NT,
+                    preferred_element_type=F32,
                 )
-                sums = sums[0:16] + sums[16:32]
-                near[r, pl.ds(8 + 64 * g + 8 * i, 8), 0:32] = sums[0:8]
-                far_sum = far_sum + sums[8:16]
-        return far_sum
+                near[r, pl.ds(pl.multiple_of(8 + 64 * g + 8 * i, 8), 8), 0:32] = sums[0:8] + sums[8:16]
+        return carry
 
     def to_rows(far_sum):
         wide = jnp.concatenate([far_sum, jnp.zeros((8, 96), F32)], axis=1)
@@ -288,6 +374,7 @@
     patch_class(3)
     group_classes()
     patch_class(2)
+    lax.fori_loop(0, 4, near_group, 0)
 
     quarter = lane8 >> 5
     blocks = []
@@ -321,6 +408,8 @@
     returned = jnp.where(half == lax.rem(s, 2), returned, 0.0)
     for copy in back_pat:
         copy.wait()
+    for on, taken, onward in relays:
+        pl.when(on)(onward.wait_send)
     incoming = [ret_pat[j] for j in range(4)] + [returned]
     left = []
     for j in range(5):
@@ -369,12 +458,13 @@
             pltpu.VMEM((5, 1, 128), F32),
             pltpu.VMEM((8, 1, 128), F32),
             pltpu.VMEM((4, 1, 128), F32),
+            pltpu.VMEM((2 * RADIUS, 1, 128), F32),
             pltpu.VMEM((8, 1, 128), F32),
             pltpu.VMEM((8, 1, 128), F32),
             pltpu.VMEM((4, 1, 128), F32),
             pltpu.SemaphoreType.DMA((7,)),
-            pltpu.SemaphoreType.DMA((32,)),
-            pltpu.SemaphoreType.DMA((32,)),
+            pltpu.SemaphoreType.DMA((40,)),
+            pltpu.SemaphoreType.DMA((40,)),
         ],
         compiler_params=pltpu.CompilerParams(
             collective_id=0, has_side_effects=True, vmem_limit_bytes=32 * 1024 * 1024

time: 21.1 us -> 18.5 us (0.88)
  the two profiles are of different devices: /device:TPU:2 before, /device:TPU:1 now
where the time goes in v4:
time: 18.5 us
  Pallas kernels  17.2 us (93%)
  between operations  0.66 us (4%)
  local copies, waits for them, and re-layouts  0.62 us (3%)
    pallas_call x1, Pallas kernels, per_device(): pl.pallas_call(functools.partial(kernel, patches, subs), out_shape=pltpu....  17.2 us
    unnamed x1, local copies, waits for them, and re-layouts  0.62 us

profile of v4, /device:TPU:1, one launch (start us, length us, event | category | flops | bytes accessed | tf_op | source)
XLA Modules:
  0.0 18.5 jit_solution(2019603108586903518)
XLA Ops:
  0.7 17.2 %divergence.1 = f32[64,128]{1,0:T(8,128)S(1)} custom-call(s32[1]{0:T(128)S(6)} %copy.10.live_hbm, f32[64,128]{1,0:T(8,128)} %bitcast.6, bf16[9,16384]{1,0:T(8,128)(2,1)} %basis_hbm.1, f32[128,128]{1,0:T(8,128)} %bitcast.5, s32[3,16384]{1,0:T(4,128)} %corners_hbm.1, s32[1,64]{1,0:T(1,128)} %bitcast.7, s32[4,128]{1,0:T(4,128)} %spat_hbm.1), custom_call_target="tpu_custom_call" | custom-call | tf_op jit(solution)/shard_map/divergence/pallas_call | solution.py:435
  17.8 0.6 %copy.9 = f32[8192]{0:T(1024)} copy(f32[8192]{0:T(1024)S(1)} %bitcast.4) | data formatting | bytes 65536

commit v5 on v4

--- a/solution.py
+++ b/solution.py
@@ -150,7 +150,7 @@
         signals = signals + here * (p >= last_row).astype(I32) * odd_core * 2 * over
     pl.semaphore_wait(barrier, signals)
 
-    forward, relays = [], []
+    forward, relays, starts = [], [], []
     for j, offset in enumerate(OFFSETS):
         copy = pltpu.make_async_remote_copy(
             src_ref=fwd_send.at[j],
@@ -162,7 +162,7 @@
         )
         forward.append(copy)
         if offset > 0:
-            copy.start()
+            starts.append(copy.start)
             continue
         slot = -offset - 1
         over, via = at < -offset, p < -offset
@@ -175,8 +175,8 @@
             device_id={"patch": lax.rem(p + last_row, patches), "sub": linked},
             device_id_type=pl.DeviceIdType.MESH,
         )
-        pl.when(via)(first.start)
-        pl.when(jnp.logical_not(via))(copy.start)
+        starts.append(functools.partial(pl.when(via), first.start))
+        starts.append(functools.partial(pl.when(jnp.logical_not(via)), copy.start))
         for kind in range(2):
             on = (odd_core == 1) & over & (p >= last_row)
             place = kind * RADIUS + slot
@@ -200,6 +200,8 @@
             taken.wait_recv()
             onward.start()
 
+    for start in reversed(starts):
+        start()
     for d in range(1, subs):
         copy = pltpu.make_async_remote_copy(
             src_ref=fwd_send.at[4],
@@ -283,8 +285,8 @@
                 values.append(jnp.where(corner >= owned, far_value, vgrp[r, g, k]))
             bas = [bgrp[r, g, i] for i in range(9)]
             grad = [bas[c] * values[0] + bas[3 + c] * values[1] + bas[6 + c] * values[2] for c in range(3)]
-            length = jnp.sqrt(grad[0] * grad[0] + grad[1] * grad[1] + grad[2] * grad[2])
-            scale = -wgrp[r, g] / jnp.maximum(length, 1.0)
+            square = grad[0] * grad[0] + grad[1] * grad[1] + grad[2] * grad[2]
+            scale = -wgrp[r, g] * lax.rsqrt(jnp.maximum(square, 1.0))
             for k in range(3):
                 term = (bas[3 * k] * grad[0] + bas[3 * k + 1] * grad[1] + bas[3 * k + 2] * grad[2]) * scale
                 high = term.astype(BF16).astype(F32)
@@ -396,8 +398,9 @@
     lane_hit, row_hit = [], []
     for j in range(5):
         index = lists[j : j + 1, :]
-        lane_hit.append(jnp.where(jnp.broadcast_to(index & 127, (128, 128)) == iota((128, 128), 0), 1.0, 0.0).astype(BF16))
-        row_hit.append(jnp.broadcast_to(index >> 7, (64, 128)) == iota((64, 128), 0))
+        column = (index & 127) + ((index >> 12) << 7)
+        lane_hit.append(jnp.where(jnp.broadcast_to(column, (256, 128)) == iota((256, 128), 0), 1.0, 0.0).astype(BF16))
+        row_hit.append(jnp.broadcast_to((index >> 7) & 31, (32, 128)) == iota((32, 128), 0))
 
     for copy in back:
         copy.wait()
@@ -418,8 +421,8 @@
         left.append(
             jnp.concatenate(
                 [
-                    jnp.where(row_hit[j], jnp.broadcast_to(high, (64, 128)), 0.0),
-                    jnp.where(row_hit[j], jnp.broadcast_to(low, (64, 128)), 0.0),
+                    jnp.where(row_hit[j], jnp.broadcast_to(high, (32, 128)), 0.0),
+                    jnp.where(row_hit[j], jnp.broadcast_to(low, (32, 128)), 0.0),
                 ],
                 axis=0,
             ).astype(BF16)
@@ -427,7 +430,9 @@
     sums = lax.dot_general(
         jnp.concatenate(left, axis=1), jnp.concatenate(lane_hit, axis=1), NT, preferred_element_type=F32
     )
-    out_ref[...] = owned_sums + (sums[0:64] + sums[64:128])
+    sums = sums[0:32] + sums[32:64]
+    out_ref[0:32, :] = owned_sums[0:32] + sums[:, 0:128]
+    out_ref[32:64, :] = owned_sums[32:64] + sums[:, 128:256]
 
 
 def per_device(patches, subs, heat, basis, area, corners, send_sub, send_pat, live_faces):

time: 18.5 us -> 18.5 us (level)
  no operation moved by 1% of the time
where the time goes in v5:
time: 18.5 us
  Pallas kernels  17.2 us (93%)
  between operations  0.66 us (4%)
  local copies, waits for them, and re-layouts  0.62 us (3%)
    pallas_call x1, Pallas kernels, per_device(): pl.pallas_call(functools.partial(kernel, patches, subs), out_shape=pltpu....  17.2 us
    unnamed x1, local copies, waits for them, and re-layouts  0.62 us

profile of v5, /device:TPU:1, one launch (start us, length us, event | category | flops | bytes accessed | tf_op | source)
XLA Modules:
  0.0 18.5 jit_solution(14368524464350293102)
XLA Ops:
  0.7 17.2 %divergence.1 = f32[64,128]{1,0:T(8,128)S(1)} custom-call(s32[1]{0:T(128)S(6)} %copy.10.live_hbm, f32[64,128]{1,0:T(8,128)} %bitcast.6, bf16[9,16384]{1,0:T(8,128)(2,1)} %basis_hbm.1, f32[128,128]{1,0:T(8,128)} %bitcast.5, s32[3,16384]{1,0:T(4,128)} %corners_hbm.1, s32[1,64]{1,0:T(1,128)} %bitcast.7, s32[4,128]{1,0:T(4,128)} %spat_hbm.1), custom_call_target="tpu_custom_call" | custom-call | tf_op jit(solution)/shard_map/divergence/pallas_call | solution.py:440
  17.8 0.6 %copy.9 = f32[8192]{0:T(1024)} copy(f32[8192]{0:T(1024)S(1)} %bitcast.4) | data formatting | bytes 65536

commit v6 on v5

--- a/solution.py
+++ b/solution.py
@@ -329,6 +329,16 @@
 
     back, back_pat = [], []
 
+    def sums_back(j):
+        return pltpu.make_async_remote_copy(
+            src_ref=ret_send.at[4 + j],
+            dst_ref=ret_pat.at[j],
+            send_sem=send_sem.at[16 + j],
+            recv_sem=recv_sem.at[16 + j],
+            device_id=peer_pat(-OFFSETS[j]),
+            device_id_type=pl.DeviceIdType.MESH,
+        )
+
     def patch_class(r):
         far = []
         for q in range(2):
@@ -337,16 +347,7 @@
         for q, row in enumerate(to_rows(one_class(r, far[0], far[1]))):
             j = 2 * (r - 2) + q
             ret_send[2 * r + q] = row
-            copy = pltpu.make_async_remote_copy(
-                src_ref=ret_send.at[2 * r + q],
-                dst_ref=ret_pat.at[j],
-                send_sem=send_sem.at[16 + j],
-                recv_sem=recv_sem.at[16 + j],
-                device_id=peer_pat(-OFFSETS[j]),
-                device_id_type=pl.DeviceIdType.MESH,
-            )
-            copy.start()
-            back_pat.append(copy)
+            sums_back(j).start()
 
     def group_classes():
         low_row = iota((1, 128), 1) < 64
@@ -373,9 +374,11 @@
             back.append(copy)
         ret_sub[s] = ret_send[s // 2]
 
-    patch_class(3)
+    pl.when(p > 0)(functools.partial(patch_class, 3))
     group_classes()
+    pl.when(p == 0)(functools.partial(patch_class, 3))
     patch_class(2)
+    back_pat.extend(sums_back(j) for j in (2, 3, 0, 1))
     lax.fori_loop(0, 4, near_group, 0)
 
     quarter = lane8 >> 5

time: 18.5 us -> 18.5 us (level)
  no operation moved by 1% of the time
where the time goes in v6:
time: 18.5 us; the launch traced here: 18.4 us
  Pallas kernels  17.1 us (92%)
  between operations  0.66 us (4%)
  local copies, waits for them, and re-layouts  0.62 us (3%)
    pallas_call x1, Pallas kernels, per_device(): pl.pallas_call(functools.partial(kernel, patches, subs), out_shape=pltpu....  17.1 us
    unnamed x1, local copies, waits for them, and re-layouts  0.62 us

profile of v6, /device:TPU:1, one launch (start us, length us, event | category | flops | bytes accessed | tf_op | source)
XLA Modules:
  0.0 18.4 jit_solution(13184250935988449069)
XLA Ops:
  0.7 17.1 %divergence.1 = f32[64,128]{1,0:T(8,128)S(1)} custom-call(s32[1]{0:T(128)S(6)} %copy.10.live_hbm, f32[64,128]{1,0:T(8,128)} %bitcast.6, bf16[9,16384]{1,0:T(8,128)(2,1)} %basis_hbm.1, f32[128,128]{1,0:T(8,128)} %bitcast.5, s32[3,16384]{1,0:T(4,128)} %corners_hbm.1, s32[1,64]{1,0:T(1,128)} %bitcast.7, s32[4,128]{1,0:T(4,128)} %spat_hbm.1), custom_call_target="tpu_custom_call" | custom-call | tf_op jit(solution)/shard_map/divergence/pallas_call | solution.py:443
  17.8 0.6 %copy.9 = f32[8192]{0:T(1024)} copy(f32[8192]{0:T(1024)S(1)} %bitcast.4) | data formatting | bytes 65536
